TPU v7x, 256 devices: a whole 4x4x8 slice. The times are simulated.
256 devices in a mesh: img: 32 (over z, x), row: 8 (over y, core).
Axes of the slice: x: 4, y: 4, z: 8, core: 2. Of those that a mesh axis runs over, the one named last changes fastest.
Arguments:
- tokens: bfloat16 [32, 64, 128, 1024], P('img', 'row'), may hold values from -14 to 14
- proj_weight: bfloat16 [1024, 256], replicated, may hold values from -0.1875 to 0.1875
- proj_bias: float32 [256], replicated, may hold values from -3 to 3
- conv_weight: bfloat16 [4, 3, 3, 256, 256], replicated, may hold values from -0.125 to 0.125
- bn_gain: float32 [4, 256], replicated, may hold values from 0.1 to 1.9
- bn_bias: float32 [4, 256], replicated, may hold values from -3 to 3
Outputs:
- joining_out: bfloat16 [32, 64, 128, 256], P('img', 'row')
All inputs are finite; a program needn't handle non-finite values.
Results may differ from a plain program's by a relative error of at most 0.0071.
Values may be sent and summed in bfloat16 or wider, within the bound.
No kernel may reach another device: no remote copies, remote signals or barrier semaphores. Data moves between devices by JAX's collectives and lax.ppermute only.
A program may use at most 64 MiB of HBM per device.

v0:
```python
import functools

import jax
import jax.numpy as jnp
from jax import lax
from jax.experimental import pallas as pl
from jax.experimental.pallas import tpu as pltpu
from jax.sharding import PartitionSpec as P


EPS = 1e-05
HALO = 4
SHAPES = {'inner': (3, 0), 'outer': (2, 0), 0: (2, 0), 1: (5, 0), 2: (2, 0)}
VM = pl.BlockSpec(memory_space=pltpu.VMEM)
HBM = pl.BlockSpec(memory_space=pltpu.HBM)
BF = jnp.bfloat16
F32 = jnp.float32
PARAMS = pltpu.CompilerParams(vmem_limit_bytes=24 << 20)
LP_PARAMS = pltpu.CompilerParams(vmem_limit_bytes=24 << 20)


def sds(shape, dtype):
    return jax.ShapeDtypeStruct(shape, dtype)


def in_hbm(x):
    return pltpu.with_memory_space_constraint(x, pltpu.HBM)


def in_vmem(x):
    return pltpu.with_memory_space_constraint(x, pltpu.VMEM)


def put_row(a3, row, x):
    cols, ch = x.shape
    col = lax.broadcasted_iota(jnp.int32, x.shape, 0)
    a3[row, :, ch : 2 * ch] = x.astype(BF)
    a3[row, :, 0:ch] = jnp.where(col == 0, 0.0, pltpu.roll(x, 1, 0)).astype(BF)
    a3[row, :, 2 * ch :] = jnp.where(col == cols - 1, 0.0, pltpu.roll(x, cols - 1, 0)).astype(BF)


def fold8(x):
    return x.reshape(-1, 8, x.shape[-1]).sum(axis=0)


def norm_terms(stats_ref, gain_ref, bias_ref, k, total):
    s = jnp.sum(stats_ref[...], axis=0)
    ch = s.shape[-1] // 2
    mean = s[:, :ch] / total
    spread = jnp.maximum(s[:, ch:] / total - mean * mean, 0.0)
    return mean, lax.rsqrt(spread + EPS) * gain_ref[k : k + 1, :], bias_ref[k : k + 1, :]


def write_stats(out_ref, sums, squares):
    both = jnp.concatenate(
        [jnp.sum(sums, axis=0, keepdims=True), jnp.sum(squares, axis=0, keepdims=True)], axis=1
    )
    out_ref[...] = jnp.broadcast_to(both[None], out_ref.shape)


def inside(local_row, strip, axis):
    if 0 <= local_row < strip:
        return None
    r = lax.axis_index(axis)
    edge = r > 0 if local_row < 0 else r < lax.axis_size(axis) - 1
    return edge.astype(F32)


def masked(x, m):
    return x if m is None else x * m


def run_conv(row_at, n_in, a3, w_parts, waits, c_ref, at, lo, strip, sums=None, squares=None, tile=(2, 0), refill=None):
    cols, ch = c_ref.shape[1:]
    n_out = n_in - 2
    step, ahead = tile
    filled = 0
    for dy in range(3):
        for copy in waits[dy]:
            copy.wait()
        w = w_parts[dy][...].reshape(3 * ch, ch)
        for done in range(0, n_out, step):
            rows = min(step, n_out - done)
            while filled < min(n_in, done + rows + dy + ahead):
                put_row(a3, filled, row_at(filled))
                filled += 1
            lhs = a3[done + dy : done + dy + rows].reshape(rows * cols, 3 * ch)
            acc = jnp.dot(lhs, w, preferred_element_type=F32)
            into = pl.ds(at + done, rows)
            if dy:
                acc = acc + c_ref[into].reshape(rows * cols, ch)
            c_ref[into] = acc.reshape(rows, cols, ch)
            own_from = max(0, -(lo + done))
            own_to = min(rows, strip - (lo + done))
            if dy == 2 and own_to > own_from:
                own = acc[own_from * cols : own_to * cols]
                s, q = fold8(own), fold8(own * own)
                sums = s if sums is None else sums + s
                squares = q if squares is None else squares + q
        if dy == 0 and refill is not None:
            refill.start()
    return sums, squares


def near_is_top(axis):
    return lax.axis_index(axis) % 2 == 1


def project(tbuf, wbuf, bbuf, out):
    y = jnp.dot(tbuf[...].reshape(-1, tbuf.shape[2]), wbuf[...], preferred_element_type=F32) + bbuf[...]
    out[...] = y.astype(BF).reshape(out.shape)


def far_proj_kernel(tok, w, bias, far, wbuf, bbuf, tbuf, sems, *, axis):
    far_at = jnp.where(near_is_top(axis), HALO, 0)
    copies = [
        pltpu.make_async_copy(w, wbuf, sems.at[0]),
        pltpu.make_async_copy(bias, bbuf, sems.at[1]),
        pltpu.make_async_copy(tok.at[pl.ds(far_at, HALO)], tbuf, sems.at[2]),
    ]
    for c in copies:
        c.start()
    for c in copies:
        c.wait()
    project(tbuf, wbuf, bbuf, far)


def near_proj_kernel(wbuf, bbuf, tok, near, tbuf, sem, *, axis):
    copy = pltpu.make_async_copy(tok.at[pl.ds(jnp.where(near_is_top(axis), 0, HALO), HALO)], tbuf, sem)
    copy.start()
    copy.wait()
    project(tbuf, wbuf, bbuf, near)


def relu_row(x):
    return jnp.maximum(x.astype(F32), 0.0)


def pick(cond, a, b):
    return jnp.where(cond, a.astype(F32), b.astype(F32))


def conv0_inner_kernel(far, near, cw, c_ref, part, w0, w_first, w_second, a3, sems, *, strip, axis):
    waits = [[pltpu.make_async_copy(cw.at[0, dy], w0.at[dy], sems.at[dy])] for dy in range(3)]
    late = [pltpu.make_async_copy(cw.at[1, dy], (w_first, w_second)[dy], sems.at[3 + dy]) for dy in range(2)]
    for copy in (*waits[0], *waits[1], *waits[2], *late):
        copy.start()
    flip = near_is_top(axis)

    def row_at(i):
        j = i % HALO
        return relu_row(pick(flip, near[j], far[j]) if i < HALO else pick(flip, far[j], near[j]))

    w_parts = [w0.at[dy] for dy in range(3)]
    part[0], part[1] = run_conv(row_at, strip, a3, w_parts, waits, c_ref, HALO, 1, strip, tile=SHAPES["inner"])
    for copy in late:
        copy.wait()


def conv0_edge(got, own, w0, part, c_ref, a3, upper, strip, exists=None):
    def theirs(i):
        return got[i] if exists is None else got[i].astype(F32) * exists

    def row_at(i):
        above = theirs(i) if i < HALO else own[i - HALO]
        below = own[i + HALO - 2] if i < 2 else theirs(i - 2)
        return relu_row(pick(upper, above, below))

    w_parts = [w0.at[dy] for dy in range(3)]
    at = jnp.where(upper, 0, strip + HALO - 2)
    run_conv(row_at, HALO + 2, a3, w_parts, [[]] * 3, c_ref, at, strip, strip, tile=SHAPES["outer"])
    row = c_ref[jnp.where(upper, HALO - 1, strip + HALO - 2)]
    return part[0] + fold8(row), part[1] + fold8(row * row)


def conv0_near_kernel(got, far, near, w0, part_in, c_in, c_ref, part, feature, a3, *, strip, axis):
    flip = near_is_top(axis)
    part[0], part[1] = conv0_edge(got, near, w0, part_in, c_ref, a3, flip, strip)
    near_at = jnp.where(flip, 0, HALO)
    feature[pl.ds(2 + near_at, HALO)] = near[...]
    feature[pl.ds(2 + HALO - near_at, HALO)] = far[...]
    feature[pl.ds(jnp.where(flip, 0, strip + 2), 2)] = got[pl.ds(jnp.where(flip, HALO - 2, 0), 2)]


def conv0_far_kernel(got, far, w0, part, c_in, feature_in, c_ref, st, feature, a3, *, strip, axis):
    flip = near_is_top(axis)
    upper = jnp.logical_not(flip)
    r = lax.axis_index(axis)
    exists = jnp.logical_and(r > 0, r < lax.axis_size(axis) - 1).astype(F32)
    sums, squares = conv0_edge(got, far, w0, part, c_ref, a3, upper, strip, exists)
    write_stats(st, sums, squares)
    feature[pl.ds(jnp.where(flip, strip + 2, 0), 2)] = got[pl.ds(jnp.where(flip, 0, HALO - 2), 2)]


def weight_copies(cw, k, parts, first, sems):
    waits = [[] for _ in parts]
    for dy in range(first, len(parts)):
        waits[dy].append(pltpu.make_async_copy(cw.at[k, dy], parts[dy], sems.at[dy - 1]))
        waits[dy][0].start()
    return waits


def hidden_conv_kernel(
    c_in, stats, gain, shift, w_first, w_second, cw, c_ref, st, *rest, k, lo, n_in, strip, total, axis
):
    *w_next, a3, wbuf, sems = rest
    refill = None
    if w_next:
        (w_first,) = w_next
        refill = pltpu.make_async_copy(cw.at[k + 2, 0], w_first, sems.at[2])
    w_parts = [w_first, w_second, wbuf.at[0]]
    waits = weight_copies(cw, k + 1, w_parts, 2, sems)
    mean, scale, bias = norm_terms(stats, gain, shift, k, total)

    def row_at(i):
        x = jnp.maximum((c_in[i] - mean) * scale + bias, 0.0)
        return masked(x, inside(lo + i, strip, axis))

    write_stats(
        st, *run_conv(row_at, n_in, a3, w_parts, waits, c_ref, 0, lo + 1, strip, tile=SHAPES[k], refill=refill)
    )
    if refill is not None:
        refill.wait()


def joined_conv_kernel(
    c_in, stats, gain, shift, w_in, feature, cw, c_ref, st, w_first, w_second, joined, a3, wbuf, sems,
    *, k, lo, n_in, strip, total, axis
):
    w_parts = [w_first, wbuf.at[0], wbuf.at[1]]
    waits = weight_copies(cw, k + 1, w_parts, 1, sems)
    late = pltpu.make_async_copy(cw.at[k + 2, 1], w_second, sems.at[3])
    late.start()
    refill = pltpu.make_async_copy(cw.at[k + 2, 0], w_first, sems.at[2])
    mean, scale, bias = norm_terms(stats, gain, shift, k, total)

    def row_at(i):
        y = (feature[i].astype(F32) + ((c_in[i] - mean) * scale + bias)).astype(BF)
        joined[i] = y
        return masked(relu_row(y), inside(lo + i, strip, axis))

    write_stats(
        st, *run_conv(row_at, n_in, a3, w_parts, waits, c_ref, 0, lo + 1, strip, tile=SHAPES[k], refill=refill)
    )
    late.wait()
    refill.wait()


def final_kernel(joined, c_in, stats, gain, shift, out, rows, sems, *, k, total):
    mean, scale, bias = norm_terms(stats, gain, shift, k, total)
    copies = []
    for i in range(0, rows.shape[0], 2):
        for j in (i, i + 1):
            rows[j] = (joined[j + 2].astype(F32) + ((c_in[j] - mean) * scale + bias)).astype(BF)
        copies.append(pltpu.make_async_copy(rows.at[i : i + 2], out.at[i : i + 2], sems.at[i // 2]))
        copies[-1].start()
    for c in copies:
        c.wait()


def sent_to_all(value, axis):
    return lax.all_to_all(value, axis, 0, 0, tiled=True)


def reduce_all(partial):
    near = sent_to_all(partial, "row").sum(axis=0)
    far = lax.axis_size("img")
    return sent_to_all(jnp.broadcast_to(near[None], (far, *near.shape)), "img")


def swapped(value, firsts):
    pairs = [(i, (i + 1) % lax.axis_size("row")) for i in firsts]
    return lax.ppermute(value, "row", pairs + [(j, i) for i, j in pairs])


def on_device(tokens, proj_weight, proj_bias, conv_weight, bn_gain, bn_bias):
    imgs, strip, cols, embed = tokens.shape
    ch = proj_weight.shape[1]
    nrow = lax.axis_size("row")
    total = float(lax.axis_size("img") * nrow * imgs * strip * cols)
    weights = in_hbm(conv_weight)
    norm_args = (bn_gain, bn_bias)

    half = sds((HALO, cols, ch), BF)
    w_third = sds((3, ch, ch), BF)
    token_rows = in_hbm(tokens[0])
    far, pw, pb = pl.pallas_call(
        functools.partial(far_proj_kernel, axis="row"),
        out_shape=(half, sds((embed, ch), BF), sds((1, ch), F32)),
        in_specs=[HBM] * 3,
        out_specs=(VM,) * 3,
        scratch_shapes=[pltpu.VMEM((HALO, cols, embed), BF), pltpu.SemaphoreType.DMA((3,))],
        compiler_params=PARAMS,
    )(token_rows, in_hbm(proj_weight), in_hbm(proj_bias[None]))
    got_far = swapped(far, range(1, nrow, 2))
    near_call = pl.pallas_call(
        functools.partial(near_proj_kernel, axis="row"),
        out_shape=half,
        in_specs=[VM, VM, HBM],
        out_specs=VM,
        scratch_shapes=[pltpu.VMEM((HALO, cols, embed), BF), pltpu.SemaphoreType.DMA(())],
        compiler_params=PARAMS,
        cost_estimate=pl.CostEstimate(
            flops=2 * embed * ch * cols * HALO, transcendentals=0, bytes_accessed=2 * HALO * cols * embed
        ),
    )
    near = near_call(in_vmem(pw), in_vmem(pb), token_rows)
    got_near = swapped(near, range(0, nrow - 1, 2))
    far, near, got_far, got_near = map(in_vmem, (far, near, got_far, got_near))

    field = sds((strip + 2 * HALO - 2, cols, ch), F32)
    stat = sds((nrow, 1, 2 * ch), F32)
    context = sds((strip + 4, cols, ch), BF)

    def rows_scratch(rows):
        return pltpu.VMEM((rows, cols, 3 * ch), BF)

    sums = sds((2, 8, ch), F32)

    def conv_flops(rows):
        return pl.CostEstimate(
            flops=2 * 9 * ch * ch * cols * rows, transcendentals=0, bytes_accessed=9 * ch * ch * 2
        )

    c, part, w0, w_first, w_second = pl.pallas_call(
        functools.partial(conv0_inner_kernel, strip=strip, axis="row"),
        out_shape=(field, sums, sds((3, 3, ch, ch), BF), w_third, w_third),
        in_specs=[VM, VM, HBM],
        out_specs=(VM,) * 5,
        scratch_shapes=[rows_scratch(strip), pltpu.SemaphoreType.DMA((5,))],
        compiler_params=PARAMS,
        cost_estimate=conv_flops(strip - 2),
    )(far, near, weights)
    w0 = in_vmem(w0)
    c, part, feature = pl.pallas_call(
        functools.partial(conv0_near_kernel, strip=strip, axis="row"),
        out_shape=(field, sums, context),
        in_specs=[VM] * 6,
        out_specs=(VM,) * 3,
        input_output_aliases={5: 0},
        scratch_shapes=[rows_scratch(HALO + 2)],
        compiler_params=PARAMS,
        cost_estimate=conv_flops(HALO),
    )(got_near, far, near, w0, in_vmem(part), in_vmem(c))
    c, st, feature = pl.pallas_call(
        functools.partial(conv0_far_kernel, strip=strip, axis="row"),
        out_shape=(field, stat, context),
        in_specs=[VM] * 6,
        out_specs=(VM,) * 3,
        input_output_aliases={4: 0, 5: 2},
        scratch_shapes=[rows_scratch(HALO + 2)],
        compiler_params=PARAMS,
        cost_estimate=conv_flops(HALO),
    )(got_far, far, w0, in_vmem(part), in_vmem(c), in_vmem(feature))

    def call(kernel, extra_in, extra_out, n_in, aliases, **kw):
        args = (in_vmem(c), in_vmem(st), *norm_args, *map(in_vmem, extra_in))
        return pl.pallas_call(
            functools.partial(kernel, n_in=n_in, strip=strip, total=total, axis="row", **kw),
            out_shape=(field, stat, *extra_out),
            in_specs=[VM] * len(args) + [HBM],
            out_specs=(VM,) * (2 + len(extra_out)),
            input_output_aliases={0: 0, **aliases},
            scratch_shapes=[
                rows_scratch(n_in),
                pltpu.VMEM((2, 3, ch, ch), BF),
                pltpu.SemaphoreType.DMA((4,)),
            ],
            compiler_params=LP_PARAMS if kernel is joined_conv_kernel else PARAMS,
        )(*args, weights)

    st = reduce_all(st)
    c, st, w_first = call(
        hidden_conv_kernel, (w_first, w_second), (w_third,), strip + 6, {4: 2}, k=0, lo=-3
    )
    st = reduce_all(st)
    c, st, w_first, w_second, joined = call(
        joined_conv_kernel, (w_first, feature), (w_third, w_third, context), strip + 4, {4: 2, 5: 4}, k=1, lo=-2
    )
    st = reduce_all(st)
    c, st = call(hidden_conv_kernel, (w_first, w_second), (), strip + 2, {}, k=2, lo=-1)
    st = reduce_all(st)
    out = pl.pallas_call(
        functools.partial(final_kernel, k=3, total=total),
        out_shape=sds((strip, cols, ch), BF),
        in_specs=[VM] * 5,
        out_specs=HBM,
        scratch_shapes=[pltpu.VMEM((strip, cols, ch), BF), pltpu.SemaphoreType.DMA((strip // 2,))],
        compiler_params=PARAMS,
    )(in_vmem(joined), in_vmem(c), in_vmem(st), *norm_args)
    return out[None]


def solution(mesh):
    placed = (P("img", "row", None, None), P(), P(), P(), P(), P())
    return jax.shard_map(
        on_device, mesh=mesh, in_specs=placed, out_specs=P("img", "row", None, None), check_vma=False
    )
```

profile of v0, /device:TPU:1, one launch (start us, length us, event | category | flops | bytes accessed | tf_op | source)
XLA Modules:
  0.0 111.7 jit_solution(11527535120872578888)
XLA Ops:
  0.0 1.9 %shard_map.64 = (bf16[4,128,256]{2,1,0:T(8,128)(2,1)S(1)}, bf16[1024,256]{1,0:T(8,128)(2,1)S(1)}, f32[1,256]{1,0:T(1,128)S(1)}) custom-call(bf16[8,128,1024]{2,1,0:T(8,128)(2,1)} %bitcast.3, bf16[1024,256]{1,0:T(8,128)(2,1)} %w.1, f32[1,256]{1,0:T(1,128)} %bitcast.5), custom_call_target="tpu_custom_call" | custom-call | tf_op jit(solution)/shard_map/pallas_call | solution.py:287
  1.9 1.7 %shard_map.65.near = bf16[4,128,256]{2,1,0:T(8,128)(2,1)S(1)} custom-call(bf16[1024,256]{1,0:T(8,128)(2,1)S(1)} %get-tuple-element.30.wbuf, f32[1,256]{1,0:T(1,128)S(1)} %get-tuple-element.31.bbuf, bf16[8,128,1024]{2,1,0:T(8,128)(2,1)} %bitcast.4), custom_call_target="tpu_custom_call" | custom-call | flops 268435456 | bytes 1048576 | tf_op jit(solution)/shard_map/pallas_call | solution.py:307
  3.6 3.3 %collective-permute-start.1 = (bf16[4,128,256]{2,1,0:T(8,128)(2,1)S(1)}, bf16[4,128,256]{2,1,0:T(8,128)(2,1)S(1)}, u32[]{:S(2)}, u32[]{:S(2)}) collective-permute-start(bf16[4,128,256]{2,1,0:T(8,128)(2,1)S(1)} %shard_map.65.near), channel_id=1, source_target_pairs={{0,1},{2,3},{4,5},{6,7},{1,0},{3,2},{5,4},{7,6},{8,9},{10,11},{12,... | collective-permute-start | bytes 786440 | tf_op jit(solution)/shard_map/ppermute | solution.py:273
  6.9 0.0 collective-permute-start
  6.9 2.3 %shard_map.66 = (f32[14,128,256]{2,1,0:T(8,128)S(1)}, f32[2,8,256]{2,1,0:T(8,128)S(1)}, bf16[3,3,256,256]{3,2,1,0:T(8,128)(2,1)S(1)}, bf16[3,256,256]{2,1,0:T(8,128)(2,1)S(1)}, bf16[3,256,256]{2,1,0:T(8,128)(2,1)S(1)}) custom-call(bf16[4,128,256]{2,1,0:T(8,128)(2,1)S(1)} %get-tuple-element.29.far, bf16[4,128,256]{2,1,0:T(8,128)(2,1)S(1)} %shard_map.65.near, ...), custom_call_target="tpu_custom_call" | custom-call | flops 905969664 | bytes 1179648 | tf_op jit(solution)/shard_map/pallas_call | solution.py:325
  9.2 0.0 collective-permute-done.1.got
  9.2 0.8 shard_map.67
  10.0 2.9 %collective-permute-done.got = bf16[4,128,256]{2,1,0:T(8,128)(2,1)S(1)} collective-permute-done((bf16[4,128,256]{2,1,0:T(8,128)(2,1)S(1)}, bf16[4,128,256]{2,1,0:T(8,128)(2,1)S(1)}, u32[]{:S(2)}, u32[]{:S(2)}) %collective-permute-start) | collective-permute-done | bytes 262176 | tf_op jit(solution)/shard_map/ppermute | solution.py:273
  12.9 0.0 copy-start
  13.0 0.0 copy-start.1
  13.0 0.9 shard_map.68
  13.8 8.1 %all_to_all.40 = f32[8,1,512]{2,1,0:T(1,128)S(1)} all-to-all(f32[8,1,512]{2,1,0:T(1,128)S(1)} %get-tuple-element.39), channel_id=1, replica_groups=mesh['img'=32,'row'=8] {'row'}, dimensions={0} | all-to-all | bytes 32768 | tf_op jit(solution)/shard_map/all_to_all | solution.py:262
  21.9 19.7 %all_to_all.41.stats = f32[32,1,512]{2,1,0:T(1,128)S(1)} all-to-all(f32[32,1,512]{2,1,0:T(1,128)S(1)} %broadcast_in_dim.13), channel_id=1, replica_groups=mesh['img'=32,'row'=8] {'img'}, dimensions={0} | all-to-all | bytes 131072 | tf_op jit(solution)/shard_map/all_to_all | solution.py:262
  41.6 0.0 copy-done
  41.6 0.0 copy-done.1
  41.6 2.2 %shard_map.69 = (f32[14,128,256]{2,1,0:T(8,128)S(1)}, f32[8,1,512]{2,1,0:T(1,128)S(1)}, bf16[3,256,256]{2,1,0:T(8,128)(2,1)S(1)}) custom-call(f32[14,128,256]{2,1,0:T(8,128)S(1)} %get-tuple-element.38.c_in, f32[32,1,512]{2,1,0:T(1,128)S(1)} %all_to_all.41.stats, f32[4,256]{1,0:T(4,128)S(1)} %copy-done, ...), custom_call_target="tpu_custom_call", output_to_operand_aliasing={{0}: (0, {}), {2}: (4, {})} | custom-call | tf_op jit(solution)/shard_map/pallas_call | solution.py:358
  43.8 9.1 %all_to_all.42 = f32[8,1,512]{2,1,0:T(1,128)S(1)} all-to-all(f32[8,1,512]{2,1,0:T(1,128)S(1)} %get-tuple-element.43), channel_id=1, replica_groups=mesh['img'=32,'row'=8] {'row'}, dimensions={0} | all-to-all | bytes 32768 | tf_op jit(solution)/shard_map/all_to_all | solution.py:262
  53.1 11.9 %all_to_all.43.stats = f32[32,1,512]{2,1,0:T(1,128)S(1)} all-to-all(f32[32,1,512]{2,1,0:T(1,128)S(1)} %broadcast_in_dim.14), channel_id=1, replica_groups=mesh['img'=32,'row'=8] {'img'}, dimensions={0} | all-to-all | bytes 131072 | tf_op jit(solution)/shard_map/all_to_all | solution.py:262
  65.0 2.3 %shard_map.70 = (f32[14,128,256]{2,1,0:T(8,128)S(1)}, f32[8,1,512]{2,1,0:T(1,128)S(1)}, bf16[3,256,256]{2,1,0:T(8,128)(2,1)S(1)}, bf16[3,256,256]{2,1,0:T(8,128)(2,1)S(1)}, bf16[12,128,256]{2,1,0:T(8,128)(2,1)S(1)}) custom-call(f32[14,128,256]{2,1,0:T(8,128)S(1)} %get-tuple-element.42.c_in, ...), custom_call_target="tpu_custom_call", output_to_operand_aliasing={{0}: (0, {}), {2}: (4, {}), {4}: (5, {})} | custom-call | tf_op jit(solution)/shard_map/pallas_call | solution.py:358
  67.3 8.9 %all_to_all.44 = f32[8,1,512]{2,1,0:T(1,128)S(1)} all-to-all(f32[8,1,512]{2,1,0:T(1,128)S(1)} %get-tuple-element.48), channel_id=1, replica_groups=mesh['img'=32,'row'=8] {'row'}, dimensions={0} | all-to-all | bytes 32768 | tf_op jit(solution)/shard_map/all_to_all | solution.py:262
  76.2 11.9 %all_to_all.45.stats = f32[32,1,512]{2,1,0:T(1,128)S(1)} all-to-all(f32[32,1,512]{2,1,0:T(1,128)S(1)} %broadcast_in_dim.15), channel_id=1, replica_groups=mesh['img'=32,'row'=8] {'img'}, dimensions={0} | all-to-all | bytes 131072 | tf_op jit(solution)/shard_map/all_to_all | solution.py:262
  88.2 1.7 %shard_map.71 = (f32[14,128,256]{2,1,0:T(8,128)S(1)}, f32[8,1,512]{2,1,0:T(1,128)S(1)}) custom-call(f32[14,128,256]{2,1,0:T(8,128)S(1)} %get-tuple-element.47.c_in, f32[32,1,512]{2,1,0:T(1,128)S(1)} %all_to_all.45.stats, f32[4,256]{1,0:T(4,128)S(1)} %copy-done, f32[4,256]{1,0:T(4,128)S(1)} %copy-done.1, ...), custom_call_target="tpu_custom_call", output_to_operand_aliasing={{0}: (0, {})} | custom-call | tf_op jit(solution)/shard_map/pallas_call | solution.py:358
  89.9 8.9 %all_to_all.46 = f32[8,1,512]{2,1,0:T(1,128)S(1)} all-to-all(f32[8,1,512]{2,1,0:T(1,128)S(1)} %get-tuple-element.52), channel_id=1, replica_groups=mesh['img'=32,'row'=8] {'row'}, dimensions={0} | all-to-all | bytes 32768 | tf_op jit(solution)/shard_map/all_to_all | solution.py:262
  98.8 11.9 %all_to_all.47.stats = f32[32,1,512]{2,1,0:T(1,128)S(1)} all-to-all(f32[32,1,512]{2,1,0:T(1,128)S(1)} %broadcast_in_dim.16), channel_id=1, replica_groups=mesh['img'=32,'row'=8] {'img'}, dimensions={0} | all-to-all | bytes 131072 | tf_op jit(solution)/shard_map/all_to_all | solution.py:262
  110.8 0.9 shard_map.72
  (8 shorter events, 0.3 us)
Async XLA Ops:
  3.6 5.6 %collective-permute-start.1 = (bf16[4,128,256]{2,1,0:T(8,128)(2,1)S(1)}, bf16[4,128,256]{2,1,0:T(8,128)(2,1)S(1)}, u32[]{:S(2)}, u32[]{:S(2)}) collective-permute-start(bf16[4,128,256]{2,1,0:T(8,128)(2,1)S(1)} %shard_map.65.near), channel_id=1, source_target_pairs={{0,1},{2,3},{4,5},{6,7},{1,0},{3,2},{5,4},{7,6},{8,9},{10,11},{12,... | collective-permute-start | bytes 786440 | tf_op jit(solution)/shard_map/ppermute | solution.py:273
  6.9 6.1 %collective-permute-start = (bf16[4,128,256]{2,1,0:T(8,128)(2,1)S(1)}, bf16[4,128,256]{2,1,0:T(8,128)(2,1)S(1)}, u32[]{:S(2)}, u32[]{:S(2)}) collective-permute-start(bf16[4,128,256]{2,1,0:T(8,128)(2,1)S(1)} %get-tuple-element.29.far), channel_id=1, source_target_pairs={{1,2},{3,4},{5,6},{7,0},{2,1},{4,3},{6,5},{0,7},{9,10},{11,12},{13... | collective-permute-start | bytes 786440 | tf_op jit(solution)/shard_map/ppermute | solution.py:273
  12.9 28.7 %copy-start = (f32[4,256]{1,0:T(4,128)S(1)}, f32[4,256]{1,0:T(4,128)}, u32[]{:S(2)}) copy-start(f32[4,256]{1,0:T(4,128)} %gain.7) | copy-start | bytes 12292
  13.0 28.7 %copy-start.1 = (f32[4,256]{1,0:T(4,128)S(1)}, f32[4,256]{1,0:T(4,128)}, u32[]{:S(2)}) copy-start(f32[4,256]{1,0:T(4,128)} %shift.7) | copy-start | bytes 12292
where the time goes:
time: 112 us
  blocking collectives  90.4 us (81%)
  Pallas kernels  14.7 us (13%)
  starting transfers between devices  3.29 us (3%)
  waiting for transfers between devices  2.92 us (3%)
    all_to_all x8, blocking collectives, sent_to_all(): return lax.all_to_all(value, axis, 0, 0, tiled=True)  90.4 us
    pallas_call x3, Pallas kernels, call(): pl.pallas_call(functools.partial(kernel, n_in=n_in, strip=strip, total=to...  6.23 us
    ppermute x2, starting transfers between devices, swapped(): return lax.ppermute(value, 'row', pairs + [(j, i) for i, j in pairs])  3.29 us
    ppermute x2, waiting for transfers between devices, swapped(): return lax.ppermute(value, 'row', pairs + [(j, i) for i, j in pairs])  2.92 us
    pallas_call x1, Pallas kernels, on_device(): pl.pallas_call(functools.partial(conv0_inner_kernel, strip=strip, axis='r...  2.31 us
  transfers between devices with their start and end apart: 2, of which 1 were waited for; matrix products, arithmetic and copies ran while one was open for 0% of the time, Pallas kernels for 3%

commit v1 on v0

--- a/solution.py
+++ b/solution.py
@@ -16,7 +16,6 @@
 BF = jnp.bfloat16
 F32 = jnp.float32
 PARAMS = pltpu.CompilerParams(vmem_limit_bytes=24 << 20)
-LP_PARAMS = pltpu.CompilerParams(vmem_limit_bytes=24 << 20)
 
 
 def sds(shape, dtype):
@@ -98,7 +97,8 @@
                 sums = s if sums is None else sums + s
                 squares = q if squares is None else squares + q
         if dy == 0 and refill is not None:
-            refill.start()
+            for copy in refill:
+                copy.start()
     return sums, squares
 
 
@@ -217,7 +217,7 @@
         return masked(x, inside(lo + i, strip, axis))
 
     write_stats(
-        st, *run_conv(row_at, n_in, a3, w_parts, waits, c_ref, 0, lo + 1, strip, tile=SHAPES[k], refill=refill)
+        st, *run_conv(row_at, n_in, a3, w_parts, waits, c_ref, 0, lo + 1, strip, tile=SHAPES[k], refill=refill and (refill,))
     )
     if refill is not None:
         refill.wait()
@@ -230,7 +230,6 @@
     w_parts = [w_first, wbuf.at[0], wbuf.at[1]]
     waits = weight_copies(cw, k + 1, w_parts, 1, sems)
     late = pltpu.make_async_copy(cw.at[k + 2, 1], w_second, sems.at[3])
-    late.start()
     refill = pltpu.make_async_copy(cw.at[k + 2, 0], w_first, sems.at[2])
     mean, scale, bias = norm_terms(stats, gain, shift, k, total)
 
@@ -240,7 +239,7 @@
         return masked(relu_row(y), inside(lo + i, strip, axis))
 
     write_stats(
-        st, *run_conv(row_at, n_in, a3, w_parts, waits, c_ref, 0, lo + 1, strip, tile=SHAPES[k], refill=refill)
+        st, *run_conv(row_at, n_in, a3, w_parts, waits, c_ref, 0, lo + 1, strip, tile=SHAPES[k], refill=(refill, late))
     )
     late.wait()
     refill.wait()
@@ -366,7 +365,7 @@
                 pltpu.VMEM((2, 3, ch, ch), BF),
                 pltpu.SemaphoreType.DMA((4,)),
             ],
-            compiler_params=LP_PARAMS if kernel is joined_conv_kernel else PARAMS,
+            compiler_params=PARAMS,
         )(*args, weights)
 
     st = reduce_all(st)

time: 112 us -> 112 us (level)
  no operation moved by 1% of the time
where the time goes in v1:
time: 112 us
  blocking collectives  90.4 us (81%)
  Pallas kernels  14.7 us (13%)
  starting transfers between devices  3.29 us (3%)
  waiting for transfers between devices  2.92 us (3%)
    all_to_all x8, blocking collectives, sent_to_all(): return lax.all_to_all(value, axis, 0, 0, tiled=True)  90.4 us
    pallas_call x3, Pallas kernels, call(): pl.pallas_call(functools.partial(kernel, n_in=n_in, strip=strip, total=to...  6.23 us
    ppermute x2, starting transfers between devices, swapped(): return lax.ppermute(value, 'row', pairs + [(j, i) for i, j in pairs])  3.29 us
    ppermute x2, waiting for transfers between devices, swapped(): return lax.ppermute(value, 'row', pairs + [(j, i) for i, j in pairs])  2.92 us
    pallas_call x1, Pallas kernels, on_device(): pl.pallas_call(functools.partial(conv0_inner_kernel, strip=strip, axis='r...  2.31 us
  transfers between devices with their start and end apart: 2, of which 1 were waited for; matrix products, arithmetic and copies ran while one was open for 0% of the time, Pallas kernels for 3%

profile of v1, /device:TPU:1, one launch (start us, length us, event | category | flops | bytes accessed | tf_op | source)
XLA Modules:
  0.0 111.7 jit_solution(5629658833264895723)
XLA Ops:
  0.0 1.9 %shard_map.64 = (bf16[4,128,256]{2,1,0:T(8,128)(2,1)S(1)}, bf16[1024,256]{1,0:T(8,128)(2,1)S(1)}, f32[1,256]{1,0:T(1,128)S(1)}) custom-call(bf16[8,128,1024]{2,1,0:T(8,128)(2,1)} %bitcast.3, bf16[1024,256]{1,0:T(8,128)(2,1)} %w.1, f32[1,256]{1,0:T(1,128)} %bitcast.5), custom_call_target="tpu_custom_call" | custom-call | tf_op jit(solution)/shard_map/pallas_call | solution.py:286
  1.9 1.7 %shard_map.65.near = bf16[4,128,256]{2,1,0:T(8,128)(2,1)S(1)} custom-call(bf16[1024,256]{1,0:T(8,128)(2,1)S(1)} %get-tuple-element.30.wbuf, f32[1,256]{1,0:T(1,128)S(1)} %get-tuple-element.31.bbuf, bf16[8,128,1024]{2,1,0:T(8,128)(2,1)} %bitcast.4), custom_call_target="tpu_custom_call" | custom-call | flops 268435456 | bytes 1048576 | tf_op jit(solution)/shard_map/pallas_call | solution.py:306
  3.6 3.3 %collective-permute-start.1 = (bf16[4,128,256]{2,1,0:T(8,128)(2,1)S(1)}, bf16[4,128,256]{2,1,0:T(8,128)(2,1)S(1)}, u32[]{:S(2)}, u32[]{:S(2)}) collective-permute-start(bf16[4,128,256]{2,1,0:T(8,128)(2,1)S(1)} %shard_map.65.near), channel_id=1, source_target_pairs={{0,1},{2,3},{4,5},{6,7},{1,0},{3,2},{5,4},{7,6},{8,9},{10,11},{12,... | collective-permute-start | bytes 786440 | tf_op jit(solution)/shard_map/ppermute | solution.py:272
  6.9 0.0 collective-permute-start
  6.9 2.3 %shard_map.66 = (f32[14,128,256]{2,1,0:T(8,128)S(1)}, f32[2,8,256]{2,1,0:T(8,128)S(1)}, bf16[3,3,256,256]{3,2,1,0:T(8,128)(2,1)S(1)}, bf16[3,256,256]{2,1,0:T(8,128)(2,1)S(1)}, bf16[3,256,256]{2,1,0:T(8,128)(2,1)S(1)}) custom-call(bf16[4,128,256]{2,1,0:T(8,128)(2,1)S(1)} %get-tuple-element.29.far, bf16[4,128,256]{2,1,0:T(8,128)(2,1)S(1)} %shard_map.65.near, ...), custom_call_target="tpu_custom_call" | custom-call | flops 905969664 | bytes 1179648 | tf_op jit(solution)/shard_map/pallas_call | solution.py:324
  9.2 0.0 collective-permute-done.1.got
  9.2 0.8 shard_map.67
  10.0 2.9 %collective-permute-done.got = bf16[4,128,256]{2,1,0:T(8,128)(2,1)S(1)} collective-permute-done((bf16[4,128,256]{2,1,0:T(8,128)(2,1)S(1)}, bf16[4,128,256]{2,1,0:T(8,128)(2,1)S(1)}, u32[]{:S(2)}, u32[]{:S(2)}) %collective-permute-start) | collective-permute-done | bytes 262176 | tf_op jit(solution)/shard_map/ppermute | solution.py:272
  12.9 0.0 copy-start
  13.0 0.0 copy-start.1
  13.0 0.9 shard_map.68
  13.8 8.1 %all_to_all.40 = f32[8,1,512]{2,1,0:T(1,128)S(1)} all-to-all(f32[8,1,512]{2,1,0:T(1,128)S(1)} %get-tuple-element.39), channel_id=1, replica_groups=mesh['img'=32,'row'=8] {'row'}, dimensions={0} | all-to-all | bytes 32768 | tf_op jit(solution)/shard_map/all_to_all | solution.py:261
  21.9 19.7 %all_to_all.41.stats = f32[32,1,512]{2,1,0:T(1,128)S(1)} all-to-all(f32[32,1,512]{2,1,0:T(1,128)S(1)} %broadcast_in_dim.13), channel_id=1, replica_groups=mesh['img'=32,'row'=8] {'img'}, dimensions={0} | all-to-all | bytes 131072 | tf_op jit(solution)/shard_map/all_to_all | solution.py:261
  41.6 0.0 copy-done
  41.6 0.0 copy-done.1
  41.6 2.2 %shard_map.69 = (f32[14,128,256]{2,1,0:T(8,128)S(1)}, f32[8,1,512]{2,1,0:T(1,128)S(1)}, bf16[3,256,256]{2,1,0:T(8,128)(2,1)S(1)}) custom-call(f32[14,128,256]{2,1,0:T(8,128)S(1)} %get-tuple-element.38.c_in, f32[32,1,512]{2,1,0:T(1,128)S(1)} %all_to_all.41.stats, f32[4,256]{1,0:T(4,128)S(1)} %copy-done, ...), custom_call_target="tpu_custom_call", output_to_operand_aliasing={{0}: (0, {}), {2}: (4, {})} | custom-call | tf_op jit(solution)/shard_map/pallas_call | solution.py:357
  43.8 9.1 %all_to_all.42 = f32[8,1,512]{2,1,0:T(1,128)S(1)} all-to-all(f32[8,1,512]{2,1,0:T(1,128)S(1)} %get-tuple-element.43), channel_id=1, replica_groups=mesh['img'=32,'row'=8] {'row'}, dimensions={0} | all-to-all | bytes 32768 | tf_op jit(solution)/shard_map/all_to_all | solution.py:261
  53.1 11.9 %all_to_all.43.stats = f32[32,1,512]{2,1,0:T(1,128)S(1)} all-to-all(f32[32,1,512]{2,1,0:T(1,128)S(1)} %broadcast_in_dim.14), channel_id=1, replica_groups=mesh['img'=32,'row'=8] {'img'}, dimensions={0} | all-to-all | bytes 131072 | tf_op jit(solution)/shard_map/all_to_all | solution.py:261
  65.0 2.3 %shard_map.70 = (f32[14,128,256]{2,1,0:T(8,128)S(1)}, f32[8,1,512]{2,1,0:T(1,128)S(1)}, bf16[3,256,256]{2,1,0:T(8,128)(2,1)S(1)}, bf16[3,256,256]{2,1,0:T(8,128)(2,1)S(1)}, bf16[12,128,256]{2,1,0:T(8,128)(2,1)S(1)}) custom-call(f32[14,128,256]{2,1,0:T(8,128)S(1)} %get-tuple-element.42.c_in, ...), custom_call_target="tpu_custom_call", output_to_operand_aliasing={{0}: (0, {}), {2}: (4, {}), {4}: (5, {})} | custom-call | tf_op jit(solution)/shard_map/pallas_call | solution.py:357
  67.3 8.9 %all_to_all.44 = f32[8,1,512]{2,1,0:T(1,128)S(1)} all-to-all(f32[8,1,512]{2,1,0:T(1,128)S(1)} %get-tuple-element.48), channel_id=1, replica_groups=mesh['img'=32,'row'=8] {'row'}, dimensions={0} | all-to-all | bytes 32768 | tf_op jit(solution)/shard_map/all_to_all | solution.py:261
  76.2 11.9 %all_to_all.45.stats = f32[32,1,512]{2,1,0:T(1,128)S(1)} all-to-all(f32[32,1,512]{2,1,0:T(1,128)S(1)} %broadcast_in_dim.15), channel_id=1, replica_groups=mesh['img'=32,'row'=8] {'img'}, dimensions={0} | all-to-all | bytes 131072 | tf_op jit(solution)/shard_map/all_to_all | solution.py:261
  88.2 1.7 %shard_map.71 = (f32[14,128,256]{2,1,0:T(8,128)S(1)}, f32[8,1,512]{2,1,0:T(1,128)S(1)}) custom-call(f32[14,128,256]{2,1,0:T(8,128)S(1)} %get-tuple-element.47.c_in, f32[32,1,512]{2,1,0:T(1,128)S(1)} %all_to_all.45.stats, f32[4,256]{1,0:T(4,128)S(1)} %copy-done, f32[4,256]{1,0:T(4,128)S(1)} %copy-done.1, ...), custom_call_target="tpu_custom_call", output_to_operand_aliasing={{0}: (0, {})} | custom-call | tf_op jit(solution)/shard_map/pallas_call | solution.py:357
  89.9 8.9 %all_to_all.46 = f32[8,1,512]{2,1,0:T(1,128)S(1)} all-to-all(f32[8,1,512]{2,1,0:T(1,128)S(1)} %get-tuple-element.52), channel_id=1, replica_groups=mesh['img'=32,'row'=8] {'row'}, dimensions={0} | all-to-all | bytes 32768 | tf_op jit(solution)/shard_map/all_to_all | solution.py:261
  98.8 11.9 %all_to_all.47.stats = f32[32,1,512]{2,1,0:T(1,128)S(1)} all-to-all(f32[32,1,512]{2,1,0:T(1,128)S(1)} %broadcast_in_dim.16), channel_id=1, replica_groups=mesh['img'=32,'row'=8] {'img'}, dimensions={0} | all-to-all | bytes 131072 | tf_op jit(solution)/shard_map/all_to_all | solution.py:261
  110.8 0.9 shard_map.72
  (8 shorter events, 0.3 us)
Async XLA Ops:
  3.6 5.6 %collective-permute-start.1 = (bf16[4,128,256]{2,1,0:T(8,128)(2,1)S(1)}, bf16[4,128,256]{2,1,0:T(8,128)(2,1)S(1)}, u32[]{:S(2)}, u32[]{:S(2)}) collective-permute-start(bf16[4,128,256]{2,1,0:T(8,128)(2,1)S(1)} %shard_map.65.near), channel_id=1, source_target_pairs={{0,1},{2,3},{4,5},{6,7},{1,0},{3,2},{5,4},{7,6},{8,9},{10,11},{12,... | collective-permute-start | bytes 786440 | tf_op jit(solution)/shard_map/ppermute | solution.py:272
  6.9 6.1 %collective-permute-start = (bf16[4,128,256]{2,1,0:T(8,128)(2,1)S(1)}, bf16[4,128,256]{2,1,0:T(8,128)(2,1)S(1)}, u32[]{:S(2)}, u32[]{:S(2)}) collective-permute-start(bf16[4,128,256]{2,1,0:T(8,128)(2,1)S(1)} %get-tuple-element.29.far), channel_id=1, source_target_pairs={{1,2},{3,4},{5,6},{7,0},{2,1},{4,3},{6,5},{0,7},{9,10},{11,12},{13... | collective-permute-start | bytes 786440 | tf_op jit(solution)/shard_map/ppermute | solution.py:272
  12.9 28.7 %copy-start = (f32[4,256]{1,0:T(4,128)S(1)}, f32[4,256]{1,0:T(4,128)}, u32[]{:S(2)}) copy-start(f32[4,256]{1,0:T(4,128)} %gain.7) | copy-start | bytes 12292
  13.0 28.7 %copy-start.1 = (f32[4,256]{1,0:T(4,128)S(1)}, f32[4,256]{1,0:T(4,128)}, u32[]{:S(2)}) copy-start(f32[4,256]{1,0:T(4,128)} %shift.7) | copy-start | bytes 12292
